TPU v7x, 32 devices: a whole 2x2x4 slice. The times are simulated.
32 devices in a mesh: com: 8 (over y, x, core), arc: 4 (over z).
Axes of the slice: x: 2, y: 2, z: 4, core: 2. Of those that a mesh axis runs over, the one named last changes fastest.
Arguments:
- flow_start: float32 [256, 65536], P('com', 'arc'), may hold values from 0 to 1
- price_start: float32 [256, 16384], P('com'), may hold values from -3 to 3
- cost: float32 [256, 65536], P('com', 'arc'), may hold values from -6 to 6
- demand: float32 [256, 16384], P('com'), may hold values from -6 to 6
- head_block: int32 [512], P('arc'), may hold values from 0 to 127
- tail_block: int32 [512], P('arc'), may hold values from 0 to 127
- head_local: int32 [65536], P('arc'), may hold values from 0 to 127
- tail_local: int32 [65536], P('arc'), may hold values from 0 to 127
- cap_class: int32 [65536], P('arc'), may hold values from 0 to 7
- cap_levels: float32 [8], replicated, may hold values from 25 to 128
Outputs:
- flow: float32 [256, 65536], P('com', 'arc')
- price: float32 [256, 16384], P('com')
Inputs may be any that keep to these rules, and one draw needn't show every extreme that they name: `head_block`: node block indices. `tail_block`: node block indices. `head_local`: positions within a node block. `tail_local`: positions within a node block.
All inputs are finite; a program needn't handle non-finite values.
Results may differ from a plain program's by a relative error of at most 0.00016.
Values sent between devices are 32-bit elements; how exact they have to be, the bound alone decides.
A program may use at most 128 MiB of HBM per device.

v0:
```python
import jax
import jax.numpy as jnp
from jax import lax
from jax.sharding import PartitionSpec as P

NODES = 16384
BLOCK = 128
CLASSES = 8
ITERS = 4
NEWTON = 3


step_primal = 0.25
step_dual = 0.1
soft_width = 0.05
highest = lax.Precision.HIGHEST


def column_sums(values, theta):
    excess = jnp.maximum(values - theta, 0.0)
    return (jnp.sum(excess, axis=0), jnp.sum(jnp.minimum(excess / soft_width, 1.0), axis=0))


def theta_step(theta, total, active, capacity):
    return theta + jnp.maximum(total - capacity, 0.0) / jnp.maximum(active, 1.0)


def on_device(
    flow_start,
    price_start,
    cost,
    demand,
    head_block,
    tail_block,
    head_local,
    tail_local,
    cap_class,
    cap_levels,
):
    com_rows, arc_cols = flow_start.shape
    blocks = arc_cols // BLOCK
    node_blocks = NODES // BLOCK
    lanes = jnp.arange(BLOCK, dtype=jnp.int32)
    head_table = (head_local.reshape(blocks, BLOCK)[:, :, None] == lanes).astype(jnp.float32)
    tail_table = (tail_local.reshape(blocks, BLOCK)[:, :, None] == lanes).astype(jnp.float32)
    block_ids = jnp.arange(node_blocks, dtype=jnp.int32)
    head_owner = (head_block[:, None] == block_ids).astype(jnp.float32)
    tail_owner = (tail_block[:, None] == block_ids).astype(jnp.float32)
    class_ids = jnp.arange(CLASSES, dtype=jnp.int32)
    capacity = jnp.sum(
        jnp.where(cap_class[:, None] == class_ids, cap_levels[None, :], 0.0), axis=1
    ).reshape(blocks, BLOCK)
    flow = flow_start.reshape(com_rows, blocks, BLOCK)
    unit_cost = cost.reshape(com_rows, blocks, BLOCK)
    price = price_start
    for step in range(ITERS):
        grid = price.reshape(com_rows, node_blocks, BLOCK)
        at_head = jnp.einsum("jn,knl->jkl", head_owner, grid, precision=highest)
        at_head = jnp.einsum("jkl,jal->kja", at_head, head_table, precision=highest)
        at_tail = jnp.einsum("jn,knl->jkl", tail_owner, grid, precision=highest)
        at_tail = jnp.einsum("jkl,jal->kja", at_tail, tail_table, precision=highest)
        trial = flow - step_primal * (unit_cost - (at_head - at_tail))
        values = lax.all_to_all(trial, "com", split_axis=1, concat_axis=0, tiled=True)
        limits = lax.all_to_all(capacity[None], "com", split_axis=1, concat_axis=0, tiled=True)
        theta = jnp.zeros(values.shape[1:], jnp.float32)
        for inner in range(NEWTON):
            total, active = column_sums(values, theta)
            theta = theta_step(theta, total, active, limits[0])
        fresh = lax.all_to_all(
            jnp.maximum(values - theta, 0.0), "com", split_axis=0, concat_axis=1, tiled=True
        )
        flows = 2.0 * fresh - flow
        inward = jnp.einsum("kja,jal->jkl", flows, head_table, precision=highest)
        inward = jnp.einsum("jn,jkl->knl", head_owner, inward, precision=highest)
        outward = jnp.einsum("kja,jal->jkl", flows, tail_table, precision=highest)
        outward = jnp.einsum("jn,jkl->knl", tail_owner, outward, precision=highest)
        balance = (inward - outward).reshape(com_rows, NODES)
        summed = lax.psum(balance, "arc")
        price = price + step_dual * (demand - summed)
        flow = fresh
    return (flow.reshape(com_rows, arc_cols), price)


def solution(mesh):
    return jax.shard_map(
        on_device,
        mesh=mesh,
        in_specs=(
            P("com", "arc"),
            P("com", None),
            P("com", "arc"),
            P("com", None),
            P("arc"),
            P("arc"),
            P("arc"),
            P("arc"),
            P("arc"),
            P(),
        ),
        out_specs=(P("com", "arc"), P("com", None)),
        check_vma=False,
    )
```

profile of v0, /device:TPU:0, one launch (start us, length us, event | category | flops | bytes accessed | tf_op | source)
XLA Modules:
  0.0 860.0 jit_solution(16881110937198093419)
XLA Ops:
  11.9 9.8 %fusion.7 = f32[128,128,32]{1,2,0:T(8,128)S(1)} fusion(s32[128,128]{1,0:T(8,128)S(1)} %bitcast.332, f32[128,32,128]{2,0,1:T(8,128)S(1)} %fusion.132), kind=kOutput, calls=%fused_computation.8 | convolution fusion | flops 807403520 | bytes 4259840 | tf_op jit(solution)/shard_map/jkl,jal->kja/dot_general | solution.py:61
  21.8 9.1 %fusion.33 = f32[32,128,128]{2,0,1:T(8,128)} fusion(f32[128,128,32]{1,2,0:T(8,128)S(1)} %fusion.7, f32[128,32,128]{2,0,1:T(8,128)S(1)} %fusion.119, s32[128,128]{1,0:T(8,128)S(1)} %bitcast.323, f32[32,16384]{1,0:T(8,128)S(1)} %copy-done, f32[32,16384]{1,0:T(8,128)S(1)} %copy-done.9), kind=kOutput, calls=%fused_computation.44 | convolution fusion | flops 809500672 | bytes 10551296 | tf_op jit(solution)/shard_map/jkl,jal->kja/dot_general | solution.py:59
  30.9 5.3 all-to-all-start
  37.1 25.8 %all-to-all-done = f32[32,128,128]{2,0,1:T(8,128)} async-done(((f32[32,128,128]{2,0,1:T(8,128)}), f32[32,128,128]{2,0,1:T(8,128)}, u32[]{:S(2)}, u32[]{:S(2)}) %all-to-all-start) | async-done | bytes 2097184 | tf_op jit(solution)/shard_map/all_to_all | solution.py:63
  62.9 3.4 all-to-all-start.1
  66.3 3.1 fusion.78
  69.4 4.1 copy.105
  73.5 3.2 fusion.82
  76.8 3.1 fusion.83
  80.1 30.9 %all_to_all.168 = f32[256,16,128]{2,1,0:T(8,128)S(1)} all-to-all(f32[256,16,128]{2,1,0:T(8,128)S(1)} %fusion.43), channel_id=1, replica_groups=mesh['com'=8,'arc'=4] {'com'}, dimensions={0} | all-to-all | bytes 4194304 | tf_op jit(solution)/shard_map/all_to_all | solution.py:69
  113.9 7.4 fusion.6
  121.3 7.5 fusion.14
  131.4 4.0 subtract_bitcast_fusion.3
  135.4 2.9 copy.110
  138.3 4.1 copy.234
  142.7 86.0 %all-reduce.5.cloned.1.call-done = f32[32,16384]{1,0:T(8,128)} async-done(((f32[32,16384]{1,0:T(8,128)}), f32[32,16384]{1,0:T(8,128)}) %all-reduce.5.cloned.1.call-update) | async-done | bytes 2097168 | tf_op jit(solution)/shard_map/psum | solution.py:78
  228.7 3.1 fusion.106
  234.7 9.8 %fusion.5 = f32[128,128,32]{1,2,0:T(8,128)S(1)} fusion(s32[128,128]{1,0:T(8,128)S(1)} %bitcast.334, f32[128,32,128]{2,0,1:T(8,128)S(1)} %fusion.129), kind=kOutput, calls=%fused_computation.6 | convolution fusion | flops 807403520 | bytes 4259840 | tf_op jit(solution)/shard_map/jkl,jal->kja/dot_general | solution.py:61
  244.6 10.2 %fusion.35 = f32[32,128,128]{2,0,1:T(8,128)S(1)} fusion(f32[32,8,16,128]{3,0,2,1:T(8,128)S(1)} %copy-done.6, f32[128,128,32]{1,2,0:T(8,128)S(1)} %fusion.5, f32[128,32,128]{2,0,1:T(8,128)S(1)} %fusion.116, s32[128,128]{1,0:T(8,128)S(1)} %bitcast.325, f32[32,16384]{1,0:T(8,128)S(1)} %copy-done), kind=kOutput, calls=%fused_computation.46 | convolution fusion | flops 809500672 | bytes 10551296 | tf_op jit(solution)/shard_map/jkl,jal->kja/dot_general | solution.py:59
  254.8 30.0 %all_to_all.169 = f32[32,128,128]{2,0,1:T(8,128)S(1)} all-to-all(f32[32,128,128]{2,0,1:T(8,128)S(1)} %fusion.35), channel_id=1, replica_groups=mesh['com'=8,'arc'=4] {'com'}, dimensions={1} | all-to-all | bytes 4194304 | tf_op jit(solution)/shard_map/all_to_all | solution.py:63
  291.1 29.2 %all_to_all.170 = f32[256,16,128]{2,1,0:T(8,128)S(1)} all-to-all(f32[256,16,128]{2,1,0:T(8,128)S(1)} %fusion.42), channel_id=1, replica_groups=mesh['com'=8,'arc'=4] {'com'}, dimensions={0} | all-to-all | bytes 4194304 | tf_op jit(solution)/shard_map/all_to_all | solution.py:69
  322.3 7.4 fusion.4
  329.7 7.5 fusion.12
  339.8 4.0 subtract_bitcast_fusion.2
  346.7 4.1 copy.233
  351.3 83.1 %all-reduce.7.cloned.1.call-done = f32[32,16384]{1,0:T(8,128)} async-done(((f32[32,16384]{1,0:T(8,128)}), f32[32,16384]{1,0:T(8,128)}) %all-reduce.7.cloned.1.call-update) | async-done | bytes 2097168 | tf_op jit(solution)/shard_map/psum | solution.py:78
  434.3 3.9 multiply_add_fusion.2
  442.1 9.8 %fusion.3 = f32[128,128,32]{1,2,0:T(8,128)S(1)} fusion(s32[128,128]{1,0:T(8,128)S(1)} %bitcast.336, f32[128,32,128]{2,0,1:T(8,128)S(1)} %fusion.126), kind=kOutput, calls=%fused_computation.4 | convolution fusion | flops 807403520 | bytes 4259840 | tf_op jit(solution)/shard_map/jkl,jal->kja/dot_general | solution.py:61
  452.0 10.2 %fusion.37 = f32[32,128,128]{2,0,1:T(8,128)S(1)} fusion(f32[32,8,16,128]{3,0,2,1:T(8,128)S(1)} %copy-done.4, f32[128,128,32]{1,2,0:T(8,128)S(1)} %fusion.3, f32[128,32,128]{2,0,1:T(8,128)S(1)} %fusion.113, s32[128,128]{1,0:T(8,128)S(1)} %bitcast.327, f32[32,16384]{1,0:T(8,128)S(1)} %copy-done), kind=kOutput, calls=%fused_computation.48 | convolution fusion | flops 809500672 | bytes 10551296 | tf_op jit(solution)/shard_map/jkl,jal->kja/dot_general | solution.py:59
  462.2 30.0 %all_to_all.171 = f32[32,128,128]{2,0,1:T(8,128)S(1)} all-to-all(f32[32,128,128]{2,0,1:T(8,128)S(1)} %fusion.37), channel_id=1, replica_groups=mesh['com'=8,'arc'=4] {'com'}, dimensions={1} | all-to-all | bytes 4194304 | tf_op jit(solution)/shard_map/all_to_all | solution.py:63
  498.5 29.2 %all_to_all.172 = f32[256,16,128]{2,1,0:T(8,128)S(1)} all-to-all(f32[256,16,128]{2,1,0:T(8,128)S(1)} %fusion.41), channel_id=1, replica_groups=mesh['com'=8,'arc'=4] {'com'}, dimensions={0} | all-to-all | bytes 4194304 | tf_op jit(solution)/shard_map/all_to_all | solution.py:69
  529.6 7.4 fusion.2
  537.0 7.5 fusion.10
  547.2 4.0 subtract_bitcast_fusion.1
  554.0 4.1 copy.232
  558.4 83.3 %all-reduce.9.cloned.1.call-done = f32[32,16384]{1,0:T(8,128)} async-done(((f32[32,16384]{1,0:T(8,128)}), f32[32,16384]{1,0:T(8,128)}) %all-reduce.9.cloned.1.call-update) | async-done | bytes 2097168 | tf_op jit(solution)/shard_map/psum | solution.py:78
  641.7 3.1 fusion.107
  647.8 9.8 %fusion.1 = f32[128,128,32]{1,2,0:T(8,128)S(1)} fusion(s32[128,128]{1,0:T(8,128)S(1)} %bitcast.338, f32[128,32,128]{2,0,1:T(8,128)S(1)} %fusion.123), kind=kOutput, calls=%fused_computation.2 | convolution fusion | flops 807403520 | bytes 4259840 | tf_op jit(solution)/shard_map/jkl,jal->kja/dot_general | solution.py:61
  657.6 10.2 %fusion.39 = f32[32,128,128]{2,0,1:T(8,128)S(1)} fusion(f32[32,8,16,128]{3,0,2,1:T(8,128)S(1)} %copy-done.2, f32[128,128,32]{1,2,0:T(8,128)S(1)} %fusion.1, f32[128,32,128]{2,0,1:T(8,128)S(1)} %fusion.110, s32[128,128]{1,0:T(8,128)S(1)} %bitcast.329, f32[32,16384]{1,0:T(8,128)S(1)} %copy-done), kind=kOutput, calls=%fused_computation.50 | convolution fusion | flops 809500672 | bytes 10551296 | tf_op jit(solution)/shard_map/jkl,jal->kja/dot_general | solution.py:59
  667.8 30.0 %all_to_all.173 = f32[32,128,128]{2,0,1:T(8,128)S(1)} all-to-all(f32[32,128,128]{2,0,1:T(8,128)S(1)} %fusion.39), channel_id=1, replica_groups=mesh['com'=8,'arc'=4] {'com'}, dimensions={1} | all-to-all | bytes 4194304 | tf_op jit(solution)/shard_map/all_to_all | solution.py:63
  704.1 29.3 %all_to_all.174 = f32[256,16,128]{2,1,0:T(8,128)S(1)} all-to-all(f32[256,16,128]{2,1,0:T(8,128)S(1)} %fusion.40), channel_id=1, replica_groups=mesh['com'=8,'arc'=4] {'com'}, dimensions={0} | all-to-all | bytes 4194304 | tf_op jit(solution)/shard_map/all_to_all | solution.py:69
  735.6 7.5 fusion
  743.1 7.5 fusion.8
  753.2 4.0 subtract_bitcast_fusion
  757.2 2.9 copy.135
  760.1 4.2 copy.230
  768.6 79.2 %all-reduce.11.cloned.1.call-done = f32[32,16384]{1,0:T(8,128)} async-done(((f32[32,16384]{1,0:T(8,128)}), f32[32,16384]{1,0:T(8,128)}) %all-reduce.11.cloned.1.call-update) | async-done | bytes 2097168 | tf_op jit(solution)/shard_map/psum | solution.py:78
  847.8 5.2 multiply_add_fusion
  (103 shorter events, 64.8 us)
Async XLA Ops:
  7.2 14.6 %copy-start = (f32[32,16384]{1,0:T(8,128)S(1)}, f32[32,16384]{1,0:T(8,128)}, u32[]{:S(2)}) copy-start(f32[32,16384]{1,0:T(8,128)} %param.12) | copy-start | bytes 6291460
  7.2 2.1 copy-start.15
  9.3 1.3 copy-start.16
  10.6 1.3 copy-start.13
  11.9 9.9 %copy-start.9 = (f32[32,16384]{1,0:T(8,128)S(1)}, f32[32,16384]{1,0:T(8,128)}, u32[]{:S(2)}) copy-start(f32[32,16384]{1,0:T(8,128)} %param.10) | copy-start | bytes 6291460
  11.9 9.9 %copy-start.12 = (s32[16384]{0:T(1024)S(1)}, s32[16384]{0:T(1024)}, u32[]{:S(2)}) copy-start(s32[16384]{0:T(1024)} %param.16) | copy-start | bytes 196612
  30.9 5.3 copy-start.14
  30.9 5.3 copy-start.17
  30.9 32.0 %all-to-all-start = ((f32[32,128,128]{2,0,1:T(8,128)}), f32[32,128,128]{2,0,1:T(8,128)}, u32[]{:S(2)}, u32[]{:S(2)}) async-start(f32[32,128,128]{2,0,1:T(8,128)} %fusion.33), calls=%async_computation | async-start | bytes 4194304 | tf_op jit(solution)/shard_map/all_to_all | solution.py:63
  62.9 10.6 %all-to-all-start.1 = ((f32[1,128,128]{2,0,1:T(1,128)}), f32[1,128,128]{2,0,1:T(1,128)S(1)}, u32[]{:S(2)}, u32[]{:S(2)}) async-start(f32[1,128,128]{2,0,1:T(1,128)} %bitcast.8), calls=%async_computation.1 | async-start | bytes 131072 | tf_op jit(solution)/shard_map/all_to_all | solution.py:64
  66.3 162.4 %all-reduce.5.cloned.1.call-start = ((), (), s32[]{:S(2)}) async-start(), calls=%async_computation.9 | async-start | bytes 4194304 | tf_op jit(solution)/shard_map/psum | solution.py:78
  73.5 6.4 copy-start.11
  111.0 1.6 copy-start.10
  112.6 1.3 copy-start.5
  142.5 291.9 %all-reduce.7.cloned.1.call-start = ((), (), s32[]{:S(2)}) async-start(), calls=%async_computation.10 | async-start | bytes 4194304 | tf_op jit(solution)/shard_map/psum | solution.py:78
  234.7 9.9 %copy-start.6 = (f32[32,8,16,128]{3,0,2,1:T(8,128)S(1)}, f32[32,8,16,128]{3,0,2,1:T(8,128)}, u32[]{:S(2)}) copy-start(f32[32,8,16,128]{3,0,2,1:T(8,128)} %copy-done.5) | copy-start | bytes 6291460
  321.0 1.3 copy-start.3
  350.8 290.9 %all-reduce.9.cloned.1.call-start = ((), (), s32[]{:S(2)}) async-start(), calls=%async_computation.11 | async-start | bytes 4194304 | tf_op jit(solution)/shard_map/psum | solution.py:78
  438.2 1.4 copy-start.7
  442.1 9.9 %copy-start.4 = (f32[32,8,16,128]{3,0,2,1:T(8,128)S(1)}, f32[32,8,16,128]{3,0,2,1:T(8,128)}, u32[]{:S(2)}) copy-start(f32[32,8,16,128]{3,0,2,1:T(8,128)} %copy-done.3) | copy-start | bytes 6291460
  528.3 1.3 copy-start.1
  558.2 289.6 %all-reduce.11.cloned.1.call-start = ((), (), s32[]{:S(2)}) async-start(), calls=%async_computation.12 | async-start | bytes 4194304 | tf_op jit(solution)/shard_map/psum | solution.py:78
  647.8 9.9 %copy-start.2 = (f32[32,8,16,128]{3,0,2,1:T(8,128)S(1)}, f32[32,8,16,128]{3,0,2,1:T(8,128)}, u32[]{:S(2)}) copy-start(f32[32,8,16,128]{3,0,2,1:T(8,128)} %copy-done.1) | copy-start | bytes 6291460
  733.4 1.3 copy-start.8
Sparse Core Ops, SparseCore 0:
  142.6 86.0 all-reduce.4
  350.9 83.3 all-reduce.6
  558.3 83.3 all-reduce.8
  764.4 83.3 all-reduce.10
where the time goes:
time: 869 us; the launch traced here: 860 us
  waiting for transfers between devices  357 us (41%)
  blocking collectives  209 us (24%)
  matrix products  175 us (20%)
  local copies, waits for them, and re-layouts  51.7 us (6%)
  other arithmetic  42.8 us (5%)
  between operations  14.9 us (2%)
  starting transfers between devices  9.63 us (1%)
    psum x4, waiting for transfers between devices, on_device(): summed = lax.psum(balance, 'arc')  331 us
    all_to_all x4, blocking collectives, on_device(): lax.all_to_all(jnp.maximum(values - theta, 0.0), 'com', split_axis=0, con...  119 us
    all_to_all x3, blocking collectives, on_device(): lax.all_to_all(trial, 'com', split_axis=1, concat_axis=0, tiled=True)  90 us
    dot_general x4, matrix products, on_device(): at_head = jnp.einsum('jkl,jal->kja', at_head, head_table, precision=highest)  39.7 us
    dot_general x4, matrix products, on_device(): at_tail = jnp.einsum('jkl,jal->kja', at_tail, tail_table, precision=highest)  39.3 us
    dot_general x4, matrix products, on_device(): inward = jnp.einsum('kja,jal->jkl', flows, head_table, precision=highest)  29.9 us
    dot_general x4, matrix products, on_device(): outward = jnp.einsum('kja,jal->jkl', flows, tail_table, precision=highest)  29.7 us
    unnamed x45, local copies, waits for them, and re-layouts  28 us
  transfers between devices with their start and end apart: 6, of which 5 were waited for; matrix products, arithmetic and copies ran while one was open for 1% of the time, Pallas kernels for 0%

commit v1 on v0

v1 whole, which is shorter than its diff:
```python
import functools

import jax
import jax.numpy as jnp
from jax import lax
from jax.experimental import pallas as pl
from jax.experimental.pallas import tpu as pltpu
from jax.sharding import PartitionSpec as P

BLOCK = 128
CLASSES = 8
ITERS = 4
NEWTON = 3
CHUNKS = 32
LAG = 2
MIB = 1 << 20

step_primal = 0.25
step_dual = 0.1
soft_width = 0.05
VMEM = pltpu.VMEM
SMEM = pltpu.SMEM
MESH = pl.DeviceIdType.MESH


def two_parts(x):
    high = x.astype(jnp.bfloat16)
    low = (x - high.astype(jnp.float32)).astype(jnp.bfloat16)
    return jnp.concatenate([high, low], axis=0)


def one_hot_rows(local_row):
    nodes = lax.broadcasted_iota(jnp.int32, (BLOCK, BLOCK), 0)
    return jnp.where(nodes == local_row, 1.0, 0.0).astype(jnp.bfloat16)


def lanes_of(block):
    return pl.ds(pl.multiple_of(block * BLOCK, BLOCK), BLOCK)


def put_sums(sums, where, within, excess):
    sums[*where, 0, pl.ds(within, 1), :] = jnp.sum(excess, axis=0, keepdims=True)
    sums[*where, 1, pl.ds(within, 1), :] = jnp.sum(
        jnp.minimum(excess * (1.0 / soft_width), 1.0), axis=0, keepdims=True
    )


def trial_kernel(
    head_block, tail_block, flow, price, cost, head_local, tail_local, trial, sums
):
    rows = flow.shape[0]
    group, _, per, _ = sums.shape
    unroll = min(per, 8)

    def some(k, carry):
        for u in range(unroll):
            block = k * unroll + u
            at_head = price[:, lanes_of(head_block[block])]
            at_tail = price[:, lanes_of(tail_block[block])]
            left = jnp.concatenate([two_parts(at_head), two_parts(at_tail)], axis=1)
            right = jnp.concatenate(
                [
                    one_hot_rows(head_local[pl.ds(block, 1), :]),
                    -one_hot_rows(tail_local[pl.ds(block, 1), :]),
                ],
                axis=0,
            )
            both = jnp.dot(left, right, preferred_element_type=jnp.float32)
            here = lanes_of(block)
            value = flow[:, here] - step_primal * (cost[:, here] - (both[:rows] + both[rows:]))
            trial[:, here] = value
            put_sums(sums, (block // per,), block % per, jnp.maximum(value, 0.0))
        return carry

    lax.fori_loop(0, group * per // unroll, some, 0)


def project_kernel(
    group,
    levels,
    trial,
    first_sums,
    cap_class,
    fresh,
    sums,
    partial,
    theta,
    sum_send,
    sum_recv,
    theta_send,
    theta_recv,
):
    me = lax.axis_index("com")
    blocks = trial.shape[1] // BLOCK
    per = blocks // group

    barrier = pltpu.get_barrier_semaphore()
    for s in range(1, group):
        pl.semaphore_signal(
            barrier, inc=1, device_id={"com": lax.rem(me + s, group)}, device_id_type=MESH
        )
    pl.semaphore_wait(barrier, group - 1)

    def own_sums(step, owner):
        return sums.at[step - 1, owner] if step else first_sums.at[owner]

    def sum_copy(step, s):
        peer = lax.rem(me + group - s, group)
        return pltpu.make_async_remote_copy(
            src_ref=own_sums(step, peer),
            dst_ref=partial.at[step, s],
            send_sem=sum_send.at[step, s],
            recv_sem=sum_recv.at[step, s],
            device_id={"com": peer},
            device_id_type=MESH,
        )

    def theta_copy(step, s):
        return pltpu.make_async_remote_copy(
            src_ref=theta.at[step, me],
            dst_ref=theta.at[step, me],
            send_sem=theta_send.at[step, s],
            recv_sem=theta_recv.at[step, s],
            device_id={"com": lax.rem(me + s, group)},
            device_id_type=MESH,
        )

    unroll = min(per, 8)

    def each_block(owner, body):
        def some(k, carry):
            for u in range(unroll):
                within = k * unroll + u
                body(owner * per + within, within)
            return carry

        lax.fori_loop(0, per // unroll, some, 0)

    for s in range(1, group):
        sum_copy(0, s).start()

    kinds = cap_class[me]
    capacity = jnp.zeros(kinds.shape, jnp.float32)
    for c in range(CLASSES):
        capacity = capacity + jnp.where(kinds == c, levels[c], 0.0)

    for step in range(NEWTON):
        both = own_sums(step, me)[...]
        for s in range(1, group):
            sum_copy(step, s).wait_recv()
            both = both + partial[step, s]
        mine = jnp.maximum(both[0] - capacity, 0.0) / jnp.maximum(both[1], 1.0)
        if step:
            mine = theta[step - 1, me] + mine
        theta[step, me] = mine
        for s in range(1, group):
            theta_copy(step, s).start()
        for s in range(group):
            owner = lax.rem(me + group - s, group)
            if s:
                theta_copy(step, s).wait_recv()

            def later(block, within, owner=owner, step=step):
                here = lanes_of(block)
                excess = jnp.maximum(
                    trial[:, here] - theta[step, owner, pl.ds(within, 1), :], 0.0
                )
                if step < NEWTON - 1:
                    put_sums(sums, (step, owner), within, excess)
                else:
                    fresh[:, here] = excess

            each_block(owner, later)
            if s and step < NEWTON - 1:
                sum_copy(step + 1, s).start()
    for step in range(NEWTON):
        for s in range(1, group):
            sum_copy(step, s).wait_send()
            theta_copy(step, s).wait_send()


def spread_kernel(head_block, tail_block, flow, fresh, head_local, tail_local, balance):
    rows = flow.shape[0]
    blocks = flow.shape[1] // BLOCK
    unroll = 8
    balance[...] = jnp.zeros_like(balance)

    def some(k, carry):
        results = []
        for u in range(unroll):
            block = k * unroll + u
            here = lanes_of(block)
            left = two_parts(2.0 * fresh[:, here] - flow[:, here])
            right = jnp.concatenate(
                [
                    one_hot_rows(head_local[pl.ds(block, 1), :]),
                    -one_hot_rows(tail_local[pl.ds(block, 1), :]),
                ],
                axis=0,
            )
            both = lax.dot_general(
                left, right, (((1,), (1,)), ((), ())), preferred_element_type=jnp.float32
            )
            results.append(both[:rows] + both[rows:])
        for u in range(unroll):
            block = k * unroll + u
            head, tail = lanes_of(head_block[block]), lanes_of(tail_block[block])
            balance[:, head] += results[u][:, :BLOCK]
            balance[:, tail] += results[u][:, BLOCK:]
        return carry

    lax.fori_loop(0, blocks // unroll, some, 0)


def price_kernel(
    line,
    balance,
    price,
    demand,
    out,
    from_left,
    from_right,
    to_right,
    to_left,
    right_send,
    right_recv,
    left_send,
    left_recv,
):
    me = lax.axis_index("arc")
    width = balance.shape[1] // CHUNKS
    first, last = me == 0, me == line - 1
    inner = jnp.logical_and(me > 0, me < line - 1)
    right, left = lax.rem(me + 1, line), lax.rem(me + line - 1, line)

    barrier = pltpu.get_barrier_semaphore()

    @pl.when(me > 0)
    def _():
        pl.semaphore_signal(barrier, inc=1, device_id={"arc": left}, device_id_type=MESH)

    @pl.when(me < line - 1)
    def _():
        pl.semaphore_signal(barrier, inc=1, device_id={"arc": right}, device_id_type=MESH)

    @pl.when(inner)
    def _():
        pl.semaphore_wait(barrier, 2)

    @pl.when(jnp.logical_not(inner))
    def _():
        pl.semaphore_wait(barrier, 1)

    def span(c):
        return pl.ds(pl.multiple_of(c * width, BLOCK), width)

    def copy(source, target, send, recv, c, peer):
        return pltpu.make_async_remote_copy(
            src_ref=source.at[:, span(c)],
            dst_ref=target.at[:, span(c)],
            send_sem=send.at[c],
            recv_sem=recv.at[c],
            device_id={"arc": peer},
            device_id_type=MESH,
        )

    def rightward(source, c):
        return copy(source, from_left, right_send, right_recv, c, right)

    def leftward(source, c):
        return copy(source, from_right, left_send, left_recv, c, left)

    def go_right(c):
        @pl.when(first)
        def _():
            rightward(balance, c).start()

        @pl.when(me > 0)
        def _():
            rightward(to_right, c).wait_recv()

        @pl.when(inner)
        def _():
            to_right[:, span(c)] = from_left[:, span(c)] + balance[:, span(c)]
            rightward(to_right, c).start()

    def go_left(c):
        @pl.when(last)
        def _():
            leftward(balance, c).start()

        @pl.when(me < line - 1)
        def _():
            leftward(to_left, c).wait_recv()

        @pl.when(inner)
        def _():
            to_left[:, span(c)] = from_right[:, span(c)] + balance[:, span(c)]
            leftward(to_left, c).start()

    def finish(c):
        def put(total):
            out[:, span(c)] = price[:, span(c)] + step_dual * (demand[:, span(c)] - total)

        @pl.when(first)
        def _():
            put(balance[:, span(c)] + from_right[:, span(c)])

        @pl.when(last)
        def _():
            put(balance[:, span(c)] + from_left[:, span(c)])

        @pl.when(inner)
        def _():
            put(to_right[:, span(c)] + from_right[:, span(c)])

    def sweep(near, far):
        for c in range(LAG):
            near(c)

        def body(c, carry):
            near(c + LAG)
            far(c)
            finish(c)
            return carry

        lax.fori_loop(0, CHUNKS - LAG, body, 0)
        for c in range(CHUNKS - LAG, CHUNKS):
            far(c)
            finish(c)

    @pl.when(me * 2 < line)
    def _():
        sweep(go_right, go_left)

    @pl.when(me * 2 >= line)
    def _():
        sweep(go_left, go_right)

    @pl.when(me < line - 1)
    def _():
        def body(c, carry):
            rightward(to_right, c).wait_send()
            return carry

        lax.fori_loop(0, CHUNKS, body, 0)

    @pl.when(me > 0)
    def _():
        def body(c, carry):
            leftward(to_left, c).wait_send()
            return carry

        lax.fori_loop(0, CHUNKS, body, 0)


def specs(*spaces):
    return [pl.BlockSpec(memory_space=space) for space in spaces]


def on_device(
    group,
    line,
    flow_start,
    price_start,
    cost,
    demand,
    head_block,
    tail_block,
    head_local,
    tail_local,
    cap_class,
    cap_levels,
):
    com_rows, arc_cols = flow_start.shape
    nodes = price_start.shape[1]
    blocks = arc_cols // BLOCK
    per = blocks // group
    heads = head_local.reshape(blocks, BLOCK)
    tails = tail_local.reshape(blocks, BLOCK)
    kinds = cap_class.reshape(group, per, BLOCK)
    dma = pltpu.SemaphoreType.DMA
    wide = jax.ShapeDtypeStruct((com_rows, arc_cols), jnp.float32)
    node = jax.ShapeDtypeStruct((com_rows, nodes), jnp.float32)

    gather = pl.pallas_call(
        trial_kernel,
        out_shape=(wide, jax.ShapeDtypeStruct((group, 2, per, BLOCK), jnp.float32)),
        in_specs=specs(SMEM, SMEM, VMEM, VMEM, VMEM, VMEM, VMEM),
        out_specs=tuple(specs(VMEM, VMEM)),
        compiler_params=pltpu.CompilerParams(vmem_limit_bytes=24 * MIB),
        name="gather",
    )
    project = pl.pallas_call(
        functools.partial(project_kernel, group),
        out_shape=wide,
        in_specs=specs(SMEM, VMEM, VMEM, VMEM),
        out_specs=pl.BlockSpec(memory_space=VMEM),
        scratch_shapes=[
            pltpu.VMEM((NEWTON - 1, group, 2, per, BLOCK), jnp.float32),
            pltpu.VMEM((NEWTON, group, 2, per, BLOCK), jnp.float32),
            pltpu.VMEM((NEWTON, group, per, BLOCK), jnp.float32),
            dma((NEWTON, group)),
            dma((NEWTON, group)),
            dma((NEWTON, group)),
            dma((NEWTON, group)),
        ],
        compiler_params=pltpu.CompilerParams(
            collective_id=0, has_side_effects=True, vmem_limit_bytes=24 * MIB
        ),
        name="project",
    )
    spread = pl.pallas_call(
        spread_kernel,
        out_shape=node,
        in_specs=specs(SMEM, SMEM, VMEM, VMEM, VMEM, VMEM),
        out_specs=pl.BlockSpec(memory_space=VMEM),
        compiler_params=pltpu.CompilerParams(vmem_limit_bytes=24 * MIB),
        name="spread",
    )
    advance = pl.pallas_call(
        functools.partial(price_kernel, line),
        out_shape=node,
        in_specs=specs(VMEM, VMEM, VMEM),
        out_specs=pl.BlockSpec(memory_space=VMEM),
        scratch_shapes=[pltpu.VMEM((com_rows, nodes), jnp.float32)] * 4
        + [dma((CHUNKS,))] * 4,
        compiler_params=pltpu.CompilerParams(
            collective_id=1, has_side_effects=True, vmem_limit_bytes=24 * MIB
        ),
        name="advance",
    )
    flow, price = flow_start, price_start
    for _ in range(ITERS):
        trial, sums = gather(head_block, tail_block, flow, price, cost, heads, tails)
        fresh = project(cap_levels, trial, sums, kinds)
        balance = spread(head_block, tail_block, flow, fresh, heads, tails)
        price = advance(balance, price, demand)
        flow = fresh
    return flow, price


def solution(mesh):
    return jax.shard_map(
        functools.partial(on_device, mesh.shape["com"], mesh.shape["arc"]),
        mesh=mesh,
        in_specs=(
            P("com", "arc"),
            P("com", None),
            P("com", "arc"),
            P("com", None),
            P("arc"),
            P("arc"),
            P("arc"),
            P("arc"),
            P("arc"),
            P(),
        ),
        out_specs=(P("com", "arc"), P("com", None)),
        check_vma=False,
    )
```

time: 869 us -> 991 us (1.14)
  Pallas kernels: 0 us -> 979 us
  waiting for transfers between devices: 357 us -> 0 us
  blocking collectives: 209 us -> 0 us
  matrix products: 175 us -> 0 us
  other arithmetic: 42.8 us -> 0 us
  local copies, waits for them, and re-layouts: 51.7 us -> 10.4 us
  between operations: 14.9 us -> 0.86 us
    pallas_call x0 -> x16, Pallas kernels: none -> 979 us  [the longest x4 841 us: on_device(): price = advance(balance, price, demand)]
    psum x4 -> x0, waiting for transfers between devices: 331 us -> none  [on_device(): summed = lax.psum(balance, 'arc')]
    all_to_all x7 -> x0, blocking collectives: 209 us -> none  [the longest x4 119 us: on_device(): lax.all_to_all(jnp.maximum(values - theta, 0.0), 'com', split_axis=0, con...]
    dot_general x32 -> x0, matrix products: 175 us -> none  [the longest x4 39.7 us: on_device(): at_head = jnp.einsum('jkl,jal->kja', at_head, head_table, precision=highest)]
    all_to_all x2 -> x0, waiting for transfers between devices: 25.8 us -> none  [the longest x1 25.8 us: on_device(): lax.all_to_all(trial, 'com', split_axis=1, concat_axis=0, tiled=True)]
    reduce_sum x13 -> x0, other arithmetic: 24.9 us -> none  [the longest x12 24 us: column_sums(): jnp.sum(excess, axis=0)]
    unnamed x45 -> x30, local copies, waits for them, and re-layouts: 28 us -> 10.4 us
    sub x4 -> x0, local copies, waits for them, and re-layouts: 11.7 us -> none  [on_device(): balance = (inward - outward).reshape(com_rows, NODES)]
  transfers between devices with their start and end apart: 6 -> 0, of which waited for: 5 -> 0; matrix products, arithmetic and copies ran while one was open for 1% -> 0% of each run, Pallas kernels for 0% -> 0%
where the time goes in v1:
time: 991 us; the launch traced here: 990 us
  Pallas kernels  979 us (99%)
  local copies, waits for them, and re-layouts  10.4 us (1%)
    pallas_call x4, Pallas kernels, on_device(): price = advance(balance, price, demand)  841 us
    pallas_call x4, Pallas kernels, on_device(): fresh = project(cap_levels, trial, sums, kinds)  94.9 us
    pallas_call x4, Pallas kernels, on_device(): balance = spread(head_block, tail_block, flow, fresh, heads, tails)  22.9 us
    pallas_call x4, Pallas kernels, on_device(): gather(head_block, tail_block, flow, price, cost, heads, tails)  20.2 us

profile of v1, /device:TPU:0, one launch (start us, length us, event | category | flops | bytes accessed | tf_op | source)
XLA Modules:
  0.0 990.5 jit_solution(13671389299736946527)
XLA Ops:
  0.6 0.0 copy-start
  0.6 1.6 copy-done
  2.2 0.0 copy-start.3
  2.2 1.6 copy-done.3
  3.8 0.0 copy-start.5
  3.8 1.6 copy-done.5
  5.4 0.0 copy-start.7
  5.4 0.8 copy-done.7
  6.2 0.0 copy-start.8
  6.3 0.8 copy-done.8
  7.1 0.0 copy-start.10
  7.1 0.7 copy-done.10
  7.7 0.0 copy-start.12
  7.7 0.7 copy-done.12
  8.4 0.0 copy-start.9
  8.4 0.0 copy-start.13
  8.4 5.1 gather.4
  13.5 0.0 copy-done.9
  13.5 0.0 copy-done.13
  13.5 0.0 copy-start.4
  13.5 25.4 %project.4.fresh.flow = f32[32,16384]{1,0:T(8,128)S(1)} custom-call(f32[8]{0:T(128)S(1)} %copy-done.13, f32[32,16384]{1,0:T(8,128)S(1)} %get-tuple-element.10.trial, f32[8,2,16,128]{3,2,1,0:T(8,128)S(1)} %get-tuple-element.11.first_sums, s32[8,16,128]{2,1,0:T(8,128)S(1)} %bitcast.19), custom_call_target="tpu_custom_call" | custom-call | tf_op jit(solution)/shard_map/project/pallas_call | solution.py:436
  38.9 0.0 copy-done.4
  38.9 0.0 copy-start.2
  38.9 0.0 copy-start.6
  38.9 5.7 spread.4.balance
  44.6 0.0 copy-done.2
  44.6 0.0 copy-done.6
  44.6 0.0 copy-start.1
  44.7 211.6 %advance.4.price = f32[32,16384]{1,0:T(8,128)S(1)} custom-call(f32[32,16384]{1,0:T(8,128)S(1)} %spread.4.balance, f32[32,16384]{1,0:T(8,128)S(1)} %copy-done.6, f32[32,16384]{1,0:T(8,128)S(1)} %copy-done.2), custom_call_target="tpu_custom_call" | custom-call | tf_op jit(solution)/shard_map/advance/pallas_call | solution.py:438
  256.3 0.0 copy-done.1
  256.3 5.1 gather.5
  261.4 0.0 copy-start.11
  261.4 23.1 %project.5.fresh.flow = f32[32,16384]{1,0:T(8,128)S(1)} custom-call(f32[8]{0:T(128)S(1)} %copy-done.13, f32[32,16384]{1,0:T(8,128)S(1)} %get-tuple-element.12.trial, f32[8,2,16,128]{3,2,1,0:T(8,128)S(1)} %get-tuple-element.13.first_sums, s32[8,16,128]{2,1,0:T(8,128)S(1)} %bitcast.20), custom_call_target="tpu_custom_call" | custom-call | tf_op jit(solution)/shard_map/project/pallas_call | solution.py:436
  284.5 0.0 copy-done.11
  284.5 5.7 spread.5.balance
  290.2 209.7 %advance.5.price = f32[32,16384]{1,0:T(8,128)S(1)} custom-call(f32[32,16384]{1,0:T(8,128)S(1)} %spread.5.balance, f32[32,16384]{1,0:T(8,128)S(1)} %advance.4.price, f32[32,16384]{1,0:T(8,128)S(1)} %copy-done.2), custom_call_target="tpu_custom_call" | custom-call | tf_op jit(solution)/shard_map/advance/pallas_call | solution.py:438
  500.0 5.1 gather.6
  505.0 23.1 %project.6.fresh.flow = f32[32,16384]{1,0:T(8,128)S(1)} custom-call(f32[8]{0:T(128)S(1)} %copy-done.13, f32[32,16384]{1,0:T(8,128)S(1)} %get-tuple-element.14.trial, f32[8,2,16,128]{3,2,1,0:T(8,128)S(1)} %get-tuple-element.15.first_sums, s32[8,16,128]{2,1,0:T(8,128)S(1)} %bitcast.21), custom_call_target="tpu_custom_call" | custom-call | tf_op jit(solution)/shard_map/project/pallas_call | solution.py:436
  528.2 5.7 spread.6.balance
  533.9 210.0 %advance.6.price = f32[32,16384]{1,0:T(8,128)S(1)} custom-call(f32[32,16384]{1,0:T(8,128)S(1)} %spread.6.balance, f32[32,16384]{1,0:T(8,128)S(1)} %advance.5.price, f32[32,16384]{1,0:T(8,128)S(1)} %copy-done.2), custom_call_target="tpu_custom_call" | custom-call | tf_op jit(solution)/shard_map/advance/pallas_call | solution.py:438
  743.9 5.1 gather.7
  748.9 23.3 %project.7.fresh = f32[32,16384]{1,0:T(8,128)S(1)} custom-call(f32[8]{0:T(128)S(1)} %copy-done.13, f32[32,16384]{1,0:T(8,128)S(1)} %get-tuple-element.16.trial, f32[8,2,16,128]{3,2,1,0:T(8,128)S(1)} %get-tuple-element.17.first_sums, s32[8,16,128]{2,1,0:T(8,128)S(1)} %bitcast.22), custom_call_target="tpu_custom_call" | custom-call | tf_op jit(solution)/shard_map/project/pallas_call | solution.py:436
  772.3 5.7 spread.7.balance
  778.0 209.8 %advance.7 = f32[32,16384]{1,0:T(8,128)S(1)} custom-call(f32[32,16384]{1,0:T(8,128)S(1)} %spread.7.balance, f32[32,16384]{1,0:T(8,128)S(1)} %advance.6.price, f32[32,16384]{1,0:T(8,128)S(1)} %copy-done.2), custom_call_target="tpu_custom_call" | custom-call | tf_op jit(solution)/shard_map/advance/pallas_call | solution.py:438
  987.8 1.3 copy.14
  989.1 1.3 copy.15
Async XLA Ops:
  0.6 1.6 copy-start
  2.2 1.6 copy-start.3
  3.8 1.6 copy-start.5
  5.4 0.8 copy-start.7
  6.2 0.8 copy-start.8
  7.1 0.7 copy-start.10
  7.7 0.7 copy-start.12
  8.4 5.1 copy-start.9
  8.4 5.1 copy-start.13
  13.5 25.4 %copy-start.4 = (f32[32,16384]{1,0:T(8,128)S(1)}, f32[32,16384]{1,0:T(8,128)}, u32[]{:S(2)}) copy-start(f32[32,16384]{1,0:T(8,128)} %flow.3) | copy-start | bytes 6291460
  38.9 5.8 copy-start.2
  38.9 5.8 copy-start.6
  44.6 211.7 %copy-start.1 = (f32[32,16384]{1,0:T(8,128)S(1)}, f32[32,16384]{1,0:T(8,128)}, u32[]{:S(2)}) copy-start(f32[32,16384]{1,0:T(8,128)} %cost.7) | copy-start | bytes 6291460
  261.4 23.1 %copy-start.11 = (s32[128]{0:T(128)S(1)}, s32[128]{0:T(128)}, u32[]{:S(2)}) copy-start(s32[128]{0:T(128)} %head_block.15) | copy-start | bytes 1540

commit v2 on v1

--- a/solution.py
+++ b/solution.py
@@ -12,7 +12,8 @@
 ITERS = 4
 NEWTON = 3
 CHUNKS = 32
-LAG = 2
+EDGE_LAG = 24
+INNER_LAG = 2
 MIB = 1 << 20
 
 step_primal = 0.25
@@ -314,28 +315,41 @@
         def _():
             put(to_right[:, span(c)] + from_right[:, span(c)])
 
-    def sweep(near, far):
-        for c in range(LAG):
+    def sweep(near, far, lag):
+        def ahead(c, carry):
             near(c)
-
-        def body(c, carry):
-            near(c + LAG)
+            return carry
+
+        def both(c, carry):
+            near(c + lag)
             far(c)
             finish(c)
             return carry
 
-        lax.fori_loop(0, CHUNKS - LAG, body, 0)
-        for c in range(CHUNKS - LAG, CHUNKS):
+        def behind(c, carry):
             far(c)
             finish(c)
-
-    @pl.when(me * 2 < line)
-    def _():
-        sweep(go_right, go_left)
-
-    @pl.when(me * 2 >= line)
-    def _():
-        sweep(go_left, go_right)
+            return carry
+
+        lax.fori_loop(0, lag, ahead, 0)
+        lax.fori_loop(0, CHUNKS - lag, both, 0)
+        lax.fori_loop(CHUNKS - lag, CHUNKS, behind, 0)
+
+    @pl.when(first)
+    def _():
+        sweep(go_right, go_left, EDGE_LAG)
+
+    @pl.when(last)
+    def _():
+        sweep(go_left, go_right, EDGE_LAG)
+
+    @pl.when(jnp.logical_and(inner, me * 2 < line))
+    def _():
+        sweep(go_right, go_left, INNER_LAG)
+
+    @pl.when(jnp.logical_and(inner, me * 2 >= line))
+    def _():
+        sweep(go_left, go_right, INNER_LAG)
 
     @pl.when(me < line - 1)
     def _():

time: 991 us -> 372 us (0.38)
  Pallas kernels: 979 us -> 360 us
    pallas_call x4, Pallas kernels: 841 us -> 222 us  [on_device(): price = advance(balance, price, demand)]
where the time goes in v2:
time: 372 us; the launch traced here: 371 us
  Pallas kernels  360 us (97%)
  local copies, waits for them, and re-layouts  10.4 us (3%)
    pallas_call x4, Pallas kernels, on_device(): price = advance(balance, price, demand)  222 us
    pallas_call x4, Pallas kernels, on_device(): fresh = project(cap_levels, trial, sums, kinds)  95 us
    pallas_call x4, Pallas kernels, on_device(): balance = spread(head_block, tail_block, flow, fresh, heads, tails)  22.9 us
    pallas_call x4, Pallas kernels, on_device(): gather(head_block, tail_block, flow, price, cost, heads, tails)  20.2 us
    unnamed x30, local copies, waits for them, and re-layouts  10.4 us

profile of v2, /device:TPU:0, one launch (start us, length us, event | category | flops | bytes accessed | tf_op | source)
XLA Modules:
  0.0 371.4 jit_solution(5490146935297347336)
XLA Ops:
  0.6 0.0 copy-start
  0.6 1.6 copy-done
  2.2 0.0 copy-start.3
  2.2 1.6 copy-done.3
  3.8 0.0 copy-start.5
  3.8 1.6 copy-done.5
  5.4 0.0 copy-start.7
  5.4 0.8 copy-done.7
  6.2 0.0 copy-start.8
  6.3 0.8 copy-done.8
  7.1 0.0 copy-start.10
  7.1 0.7 copy-done.10
  7.7 0.0 copy-start.12
  7.7 0.7 copy-done.12
  8.4 0.0 copy-start.9
  8.4 0.0 copy-start.13
  8.4 5.1 %gather.4 = (f32[32,16384]{1,0:T(8,128)S(1)}, f32[8,2,16,128]{3,2,1,0:T(8,128)S(1)}) custom-call(s32[128]{0:T(128)S(1)} %copy-done.10, s32[128]{0:T(128)S(1)} %copy-done.12, f32[32,16384]{1,0:T(8,128)S(1)} %copy-done.3, f32[32,16384]{1,0:T(8,128)S(1)} %copy-done.5, f32[32,16384]{1,0:T(8,128)S(1)} %copy-done, s32[128,128]{1,0:T(8,128)S(1)} %bitcast.3, ...), custom_call_target="tpu_custom_call" | custom-call | tf_op jit(solution)/shard_map/gather/pallas_call | solution.py:449
  13.5 0.0 copy-done.9
  13.5 0.0 copy-done.13
  13.5 0.0 copy-start.4
  13.5 25.4 %project.4.fresh.flow = f32[32,16384]{1,0:T(8,128)S(1)} custom-call(f32[8]{0:T(128)S(1)} %copy-done.13, f32[32,16384]{1,0:T(8,128)S(1)} %get-tuple-element.10.trial, f32[8,2,16,128]{3,2,1,0:T(8,128)S(1)} %get-tuple-element.11.first_sums, s32[8,16,128]{2,1,0:T(8,128)S(1)} %bitcast.19), custom_call_target="tpu_custom_call" | custom-call | tf_op jit(solution)/shard_map/project/pallas_call | solution.py:450
  38.9 0.0 copy-done.4
  38.9 0.0 copy-start.2
  38.9 0.0 copy-start.6
  38.9 5.7 %spread.4.balance = f32[32,16384]{1,0:T(8,128)S(1)} custom-call(s32[128]{0:T(128)S(1)} %copy-done.10, s32[128]{0:T(128)S(1)} %copy-done.12, f32[32,16384]{1,0:T(8,128)S(1)} %copy-done.4, f32[32,16384]{1,0:T(8,128)S(1)} %project.4.fresh.flow, s32[128,128]{1,0:T(8,128)S(1)} %bitcast.4, s32[128,128]{1,0:T(8,128)S(1)} %bitcast.12), custom_call_target="tpu_custom_call" | custom-call | tf_op jit(solution)/shard_map/spread/pallas_call | solution.py:451
  44.6 0.0 copy-done.2
  44.6 0.0 copy-done.6
  44.7 0.0 copy-start.1
  44.7 57.3 %advance.4.price = f32[32,16384]{1,0:T(8,128)S(1)} custom-call(f32[32,16384]{1,0:T(8,128)S(1)} %spread.4.balance, f32[32,16384]{1,0:T(8,128)S(1)} %copy-done.6, f32[32,16384]{1,0:T(8,128)S(1)} %copy-done.2), custom_call_target="tpu_custom_call" | custom-call | tf_op jit(solution)/shard_map/advance/pallas_call | solution.py:452
  102.0 0.0 copy-done.1
  102.0 5.1 %gather.5 = (f32[32,16384]{1,0:T(8,128)S(1)}, f32[8,2,16,128]{3,2,1,0:T(8,128)S(1)}) custom-call(s32[128]{0:T(128)S(1)} %copy-done.10, s32[128]{0:T(128)S(1)} %copy-done.12, f32[32,16384]{1,0:T(8,128)S(1)} %project.4.fresh.flow, f32[32,16384]{1,0:T(8,128)S(1)} %advance.4.price, f32[32,16384]{1,0:T(8,128)S(1)} %copy-done.1, s32[128,128]{1,0:T(8,128)S(1)} %bitcast.5, ...), custom_call_target="tpu_custom_call" | custom-call | tf_op jit(solution)/shard_map/gather/pallas_call | solution.py:449
  107.0 0.0 copy-start.11
  107.0 23.1 %project.5.fresh.flow = f32[32,16384]{1,0:T(8,128)S(1)} custom-call(f32[8]{0:T(128)S(1)} %copy-done.13, f32[32,16384]{1,0:T(8,128)S(1)} %get-tuple-element.12.trial, f32[8,2,16,128]{3,2,1,0:T(8,128)S(1)} %get-tuple-element.13.first_sums, s32[8,16,128]{2,1,0:T(8,128)S(1)} %bitcast.20), custom_call_target="tpu_custom_call" | custom-call | tf_op jit(solution)/shard_map/project/pallas_call | solution.py:450
  130.1 0.0 copy-done.11
  130.1 5.7 %spread.5.balance = f32[32,16384]{1,0:T(8,128)S(1)} custom-call(s32[128]{0:T(128)S(1)} %copy-done.11, s32[128]{0:T(128)S(1)} %copy-done.12, f32[32,16384]{1,0:T(8,128)S(1)} %project.4.fresh.flow, f32[32,16384]{1,0:T(8,128)S(1)} %project.5.fresh.flow, s32[128,128]{1,0:T(8,128)S(1)} %bitcast.6, s32[128,128]{1,0:T(8,128)S(1)} %bitcast.14), custom_call_target="tpu_custom_call" | custom-call | tf_op jit(solution)/shard_map/spread/pallas_call | solution.py:451
  135.9 54.8 %advance.5.price = f32[32,16384]{1,0:T(8,128)S(1)} custom-call(f32[32,16384]{1,0:T(8,128)S(1)} %spread.5.balance, f32[32,16384]{1,0:T(8,128)S(1)} %advance.4.price, f32[32,16384]{1,0:T(8,128)S(1)} %copy-done.2), custom_call_target="tpu_custom_call" | custom-call | tf_op jit(solution)/shard_map/advance/pallas_call | solution.py:452
  190.7 5.1 %gather.6 = (f32[32,16384]{1,0:T(8,128)S(1)}, f32[8,2,16,128]{3,2,1,0:T(8,128)S(1)}) custom-call(s32[128]{0:T(128)S(1)} %copy-done.11, s32[128]{0:T(128)S(1)} %copy-done.12, f32[32,16384]{1,0:T(8,128)S(1)} %project.5.fresh.flow, f32[32,16384]{1,0:T(8,128)S(1)} %advance.5.price, f32[32,16384]{1,0:T(8,128)S(1)} %copy-done.1, s32[128,128]{1,0:T(8,128)S(1)} %bitcast.7, ...), custom_call_target="tpu_custom_call" | custom-call | tf_op jit(solution)/shard_map/gather/pallas_call | solution.py:449
  195.8 23.3 %project.6.fresh.flow = f32[32,16384]{1,0:T(8,128)S(1)} custom-call(f32[8]{0:T(128)S(1)} %copy-done.13, f32[32,16384]{1,0:T(8,128)S(1)} %get-tuple-element.14.trial, f32[8,2,16,128]{3,2,1,0:T(8,128)S(1)} %get-tuple-element.15.first_sums, s32[8,16,128]{2,1,0:T(8,128)S(1)} %bitcast.21), custom_call_target="tpu_custom_call" | custom-call | tf_op jit(solution)/shard_map/project/pallas_call | solution.py:450
  219.0 5.7 %spread.6.balance = f32[32,16384]{1,0:T(8,128)S(1)} custom-call(s32[128]{0:T(128)S(1)} %copy-done.11, s32[128]{0:T(128)S(1)} %copy-done.12, f32[32,16384]{1,0:T(8,128)S(1)} %project.5.fresh.flow, f32[32,16384]{1,0:T(8,128)S(1)} %project.6.fresh.flow, s32[128,128]{1,0:T(8,128)S(1)} %bitcast.8, s32[128,128]{1,0:T(8,128)S(1)} %bitcast.16), custom_call_target="tpu_custom_call" | custom-call | tf_op jit(solution)/shard_map/spread/pallas_call | solution.py:451
  224.8 55.2 %advance.6.price = f32[32,16384]{1,0:T(8,128)S(1)} custom-call(f32[32,16384]{1,0:T(8,128)S(1)} %spread.6.balance, f32[32,16384]{1,0:T(8,128)S(1)} %advance.5.price, f32[32,16384]{1,0:T(8,128)S(1)} %copy-done.2), custom_call_target="tpu_custom_call" | custom-call | tf_op jit(solution)/shard_map/advance/pallas_call | solution.py:452
  280.0 5.1 %gather.7 = (f32[32,16384]{1,0:T(8,128)S(1)}, f32[8,2,16,128]{3,2,1,0:T(8,128)S(1)}) custom-call(s32[128]{0:T(128)S(1)} %copy-done.11, s32[128]{0:T(128)S(1)} %copy-done.12, f32[32,16384]{1,0:T(8,128)S(1)} %project.6.fresh.flow, f32[32,16384]{1,0:T(8,128)S(1)} %advance.6.price, f32[32,16384]{1,0:T(8,128)S(1)} %copy-done.1, s32[128,128]{1,0:T(8,128)S(1)} %bitcast.9, ...), custom_call_target="tpu_custom_call" | custom-call | tf_op jit(solution)/shard_map/gather/pallas_call | solution.py:449
  285.0 23.3 %project.7.fresh = f32[32,16384]{1,0:T(8,128)S(1)} custom-call(f32[8]{0:T(128)S(1)} %copy-done.13, f32[32,16384]{1,0:T(8,128)S(1)} %get-tuple-element.16.trial, f32[8,2,16,128]{3,2,1,0:T(8,128)S(1)} %get-tuple-element.17.first_sums, s32[8,16,128]{2,1,0:T(8,128)S(1)} %bitcast.22), custom_call_target="tpu_custom_call" | custom-call | tf_op jit(solution)/shard_map/project/pallas_call | solution.py:450
  308.4 5.7 %spread.7.balance = f32[32,16384]{1,0:T(8,128)S(1)} custom-call(s32[128]{0:T(128)S(1)} %copy-done.11, s32[128]{0:T(128)S(1)} %copy-done.12, f32[32,16384]{1,0:T(8,128)S(1)} %project.6.fresh.flow, f32[32,16384]{1,0:T(8,128)S(1)} %project.7.fresh, s32[128,128]{1,0:T(8,128)S(1)} %bitcast.10, s32[128,128]{1,0:T(8,128)S(1)} %bitcast.18), custom_call_target="tpu_custom_call" | custom-call | tf_op jit(solution)/shard_map/spread/pallas_call | solution.py:451
  314.1 54.7 %advance.7 = f32[32,16384]{1,0:T(8,128)S(1)} custom-call(f32[32,16384]{1,0:T(8,128)S(1)} %spread.7.balance, f32[32,16384]{1,0:T(8,128)S(1)} %advance.6.price, f32[32,16384]{1,0:T(8,128)S(1)} %copy-done.2), custom_call_target="tpu_custom_call" | custom-call | tf_op jit(solution)/shard_map/advance/pallas_call | solution.py:452
  368.8 1.3 copy.14
  370.1 1.3 copy.15
Async XLA Ops:
  0.6 1.6 copy-start
  2.2 1.6 copy-start.3
  3.8 1.6 copy-start.5
  5.4 0.8 copy-start.7
  6.2 0.8 copy-start.8
  7.1 0.7 copy-start.10
  7.7 0.7 copy-start.12
  8.4 5.1 %copy-start.9 = (s32[16384]{0:T(1024)S(1)}, s32[16384]{0:T(1024)}, u32[]{:S(2)}) copy-start(s32[16384]{0:T(1024)} %param.18) | copy-start | bytes 196612
  8.4 5.1 %copy-start.13 = (f32[8]{0:T(128)S(1)}, f32[8]{0:T(128)}, u32[]{:S(2)}) copy-start(f32[8]{0:T(128)} %levels.7) | copy-start | bytes 100
  13.5 25.4 %copy-start.4 = (f32[32,16384]{1,0:T(8,128)S(1)}, f32[32,16384]{1,0:T(8,128)}, u32[]{:S(2)}) copy-start(f32[32,16384]{1,0:T(8,128)} %flow.3) | copy-start | bytes 6291460
  38.9 5.8 %copy-start.2 = (f32[32,16384]{1,0:T(8,128)S(1)}, f32[32,16384]{1,0:T(8,128)}, u32[]{:S(2)}) copy-start(f32[32,16384]{1,0:T(8,128)} %demand.7) | copy-start | bytes 6291460
  38.9 5.8 %copy-start.6 = (f32[32,16384]{1,0:T(8,128)S(1)}, f32[32,16384]{1,0:T(8,128)}, u32[]{:S(2)}) copy-start(f32[32,16384]{1,0:T(8,128)} %price.3) | copy-start | bytes 6291460
  44.7 57.3 %copy-start.1 = (f32[32,16384]{1,0:T(8,128)S(1)}, f32[32,16384]{1,0:T(8,128)}, u32[]{:S(2)}) copy-start(f32[32,16384]{1,0:T(8,128)} %cost.7) | copy-start | bytes 6291460
  107.0 23.1 %copy-start.11 = (s32[128]{0:T(128)S(1)}, s32[128]{0:T(128)}, u32[]{:S(2)}) copy-start(s32[128]{0:T(128)} %head_block.15) | copy-start | bytes 1540
